TPU v7x, 32 devices: a whole 2x2x4 slice. The times are simulated.
32 devices in a mesh: seq: 16 (over z, y, core), head: 2 (over x).
Axes of the slice: x: 2, y: 2, z: 4, core: 2. Of those that a mesh axis runs over, the one named last changes fastest.
Arguments:
- queries: bfloat16 [4096, 4096], P('seq', 'head'), may hold values from -8 to 8
- keys: bfloat16 [4096, 2048], P('seq', 'head'), may hold values from -8 to 8
- values: bfloat16 [4096, 2048], P('seq', 'head'), may hold values from -6 to 6
- segment_ids: int32 [4096], P(('seq', 'head')), may hold values from 0 to 7, never falling along the last dimension, each value on 1 to 2048 neighbouring positions
Outputs:
- attended: bfloat16 [4096, 4096], P('seq', 'head')
Inputs may be any that keep to these rules, and one draw needn't show every extreme that they name: `segment_ids`: document numbers never fall along the tokens; each document has 1 to 2048 tokens, one exactly 2048.
All inputs are finite; a program needn't handle non-finite values.
Results may differ from a plain program's by a relative error of at most 0.0037.
Values may be sent and summed in bfloat16 or wider, within the bound.
No kernel may reach another device: no remote copies, remote signals or barrier semaphores. Data moves between devices by JAX's collectives and lax.ppermute only.
A program may use at most 64 MiB of HBM per device.

v0:
```python
import jax
import jax.numpy as jnp
from jax import lax
from jax.sharding import PartitionSpec as P

HEAD_WIDTH = 128
WINDOW = 1024


score_scale = 168.0 ** (-0.5)


def from_behind(value, axis, steps):
    count = lax.axis_size(axis)
    initial, last = (max(0, -steps), min(count, count - steps))
    return lax.ppermute(value, axis, [(source, source + steps) for source in range(initial, last)])


def attend(queries, keys, values, query_ids, key_ids, query_pos, key_pos):
    tok_rows = queries.shape[0]
    span = keys.shape[0]
    kv_heads = keys.shape[1] // HEAD_WIDTH
    group = queries.shape[1] // keys.shape[1]
    visible = (
        (key_ids[None, :] == query_ids[:, None])
        & (key_pos[None, :] <= query_pos[:, None])
        & (query_pos[:, None] - key_pos[None, :] < WINDOW)
    )
    grouped_q = queries.reshape(tok_rows, kv_heads, group, HEAD_WIDTH).transpose(1, 0, 2, 3)
    grouped_k = keys.reshape(span, kv_heads, HEAD_WIDTH).transpose(1, 0, 2)
    grouped_v = values.reshape(span, kv_heads, HEAD_WIDTH).transpose(1, 0, 2)

    def one_head(operands):
        head_q, head_k, head_v = operands
        scores = (
            jnp.einsum("tgd,sd->gts", head_q, head_k, preferred_element_type=jnp.float32)
            * score_scale
        )
        scores = jnp.where(visible[None], scores, -1e30)
        top = jnp.max(scores, axis=2, keepdims=True)
        weights = jnp.exp(scores - top)
        total = jnp.sum(weights, axis=2)
        rounded = weights.astype(jnp.bfloat16)
        mixed = jnp.einsum("gts,sd->tgd", rounded, head_v, preferred_element_type=jnp.float32)
        return (mixed / total.T[:, :, None]).astype(jnp.bfloat16)

    final_output = lax.map(one_head, (grouped_q, grouped_k, grouped_v))
    return final_output.transpose(1, 0, 2, 3).reshape(tok_rows, -1)


def body(queries, keys, values, segment_ids):
    own_ids = lax.all_gather(segment_ids, "head", axis=0, tiled=True)
    tok_rows = keys.shape[0]
    reach = WINDOW // tok_rows
    tagged = own_ids + 1
    packet = (keys, values, tagged)
    received = []
    for distance in range(reach):
        received.append(from_behind((packet[0], packet[1], packet[2]), "seq", distance + 1))
    ordered = list(reversed(received)) + [packet]
    all_keys = jnp.concatenate([piece[0] for piece in ordered], axis=0)
    all_values = jnp.concatenate([piece[1] for piece in ordered], axis=0)
    key_ids = jnp.concatenate([piece[2] for piece in ordered], axis=0) - 1
    query_pos = jnp.arange(tok_rows, dtype=jnp.int32)
    key_pos = jnp.arange(all_keys.shape[0], dtype=jnp.int32) - reach * tok_rows
    return attend(queries, all_keys, all_values, own_ids, key_ids, query_pos, key_pos)


def solution(mesh):
    in_specs = (P("seq", "head"), P("seq", "head"), P("seq", "head"), P(("seq", "head")))
    out_specs = P("seq", "head")
    return jax.shard_map(body, mesh=mesh, in_specs=in_specs, out_specs=out_specs, check_vma=False)
```

profile of v0, /device:TPU:10, one launch (start us, length us, event | category | flops | bytes accessed | tf_op | source)
XLA Modules:
  0.0 142.4 jit_solution(7033362159586849298)
XLA Ops:
  0.0 4.5 %all-gather = s32[2,1,128]{2,1,0:T(1,128)S(1)} all-gather(s32[1,1,128]{2,1,0:T(1,128)} %bitcast.69), channel_id=1, replica_groups=mesh['seq'=16,'head'=2] {'head'}, dimensions={0}, use_global_device_ids=true | all-gather | bytes 1536 | tf_op jit(solution)/shard_map/all_gather | solution.py:52
  4.5 3.5 %collective-permute-start.4 = (s32[256]{0:T(256)S(1)}, s32[256]{0:T(256)S(1)}, u32[]{:S(2)}, u32[]{:S(2)}) collective-permute-start(s32[256]{0:T(256)S(1)} %broadcast_add_fusion.1), channel_id=1, source_target_pairs={{0,8},{2,10},{4,12},{6,14},{8,16},{10,18},{12,20},{14,22},{16,24},... | collective-permute-start | bytes 3080 | tf_op jit(solution)/shard_map/ppermute | solution.py:16
  8.0 1.9 %collective-permute-start.5 = (s32[256]{0:T(256)S(1)}, s32[256]{0:T(256)S(1)}, u32[]{:S(2)}, u32[]{:S(2)}) collective-permute-start(s32[256]{0:T(256)S(1)} %broadcast_add_fusion.1), channel_id=1, source_target_pairs={{0,6},{2,8},{4,10},{6,12},{8,14},{10,16},{12,18},{14,20},{16,22},{... | collective-permute-start | bytes 3080 | tf_op jit(solution)/shard_map/ppermute | solution.py:16
  9.9 3.4 %collective-permute-start.6 = (s32[256]{0:T(256)S(1)}, s32[256]{0:T(256)S(1)}, u32[]{:S(2)}, u32[]{:S(2)}) collective-permute-start(s32[256]{0:T(256)S(1)} %broadcast_add_fusion.1), channel_id=1, source_target_pairs={{0,4},{2,6},{4,8},{6,10},{8,12},{10,14},{12,16},{14,18},{16,20},{1... | collective-permute-start | bytes 3080 | tf_op jit(solution)/shard_map/ppermute | solution.py:16
  13.3 3.3 %collective-permute-start.7 = (s32[256]{0:T(256)S(1)}, s32[256]{0:T(256)S(1)}, u32[]{:S(2)}, u32[]{:S(2)}) collective-permute-start(s32[256]{0:T(256)S(1)} %broadcast_add_fusion.1), channel_id=1, source_target_pairs={{0,2},{2,4},{4,6},{6,8},{8,10},{10,12},{12,14},{14,16},{16,18},{18... | collective-permute-start | bytes 3080 | tf_op jit(solution)/shard_map/ppermute | solution.py:16
  16.7 1.2 copy.21
  17.9 2.1 %collective-permute-start.8 = (bf16[256,1024]{0,1:T(8,128)(2,1)S(1)}, bf16[256,1024]{0,1:T(8,128)(2,1)S(1)}, u32[]{:S(2)}, u32[]{:S(2)}) collective-permute-start(bf16[256,1024]{0,1:T(8,128)(2,1)S(1)} %copy.21), channel_id=1, source_target_pairs={{0,8},{2,10},{4,12},{6,14},{8,16},{10,18},{12,20},{14,22},{16,24},... | collective-permute-start | bytes 1572872 | tf_op jit(solution)/shard_map/ppermute | solution.py:16
  20.0 2.3 %copy.26 = bf16[256,2048]{0,1:T(8,128)(2,1)} copy(bf16[256,2048]{1,0:T(8,128)(2,1)} %param.6) | data formatting | bytes 2097152 | tf_op args[0]
  22.3 0.0 collective-permute-done.4
  22.3 3.1 %collective-permute-start.9 = (bf16[256,1024]{0,1:T(8,128)(2,1)S(1)}, bf16[256,1024]{0,1:T(8,128)(2,1)S(1)}, u32[]{:S(2)}, u32[]{:S(2)}) collective-permute-start(bf16[256,1024]{0,1:T(8,128)(2,1)S(1)} %copy.21), channel_id=1, source_target_pairs={{0,6},{2,8},{4,10},{6,12},{8,14},{10,16},{12,18},{14,20},{16,22},{... | collective-permute-start | bytes 1572872 | tf_op jit(solution)/shard_map/ppermute | solution.py:16
  25.4 0.0 collective-permute-done.5
  25.4 1.9 %collective-permute-start.10 = (bf16[256,1024]{0,1:T(8,128)(2,1)S(1)}, bf16[256,1024]{0,1:T(8,128)(2,1)S(1)}, u32[]{:S(2)}, u32[]{:S(2)}) collective-permute-start(bf16[256,1024]{0,1:T(8,128)(2,1)S(1)} %copy.21), channel_id=1, source_target_pairs={{0,4},{2,6},{4,8},{6,10},{8,12},{10,14},{12,16},{14,18},{16,20},{1... | collective-permute-start | bytes 1572872 | tf_op jit(solution)/shard_map/ppermute | solution.py:16
  27.4 2.0 %collective-permute-start.11 = (bf16[256,1024]{0,1:T(8,128)(2,1)S(1)}, bf16[256,1024]{0,1:T(8,128)(2,1)S(1)}, u32[]{:S(2)}, u32[]{:S(2)}) collective-permute-start(bf16[256,1024]{0,1:T(8,128)(2,1)S(1)} %copy.21), channel_id=1, source_target_pairs={{0,2},{2,4},{4,6},{6,8},{8,10},{10,12},{12,14},{14,16},{16,18},{18... | collective-permute-start | bytes 1572872 | tf_op jit(solution)/shard_map/ppermute | solution.py:16
  29.4 0.0 collective-permute-done.7
  29.4 1.9 %collective-permute-start = (bf16[256,1024]{1,0:T(8,128)(2,1)S(1)}, bf16[256,1024]{1,0:T(8,128)(2,1)S(1)}, u32[]{:S(2)}, u32[]{:S(2)}) collective-permute-start(bf16[256,1024]{1,0:T(8,128)(2,1)S(1)} %copy-done), channel_id=1, source_target_pairs={{0,8},{2,10},{4,12},{6,14},{8,16},{10,18},{12,20},{14,22},{16,24},... | collective-permute-start | bytes 1572872 | tf_op jit(solution)/shard_map/ppermute | solution.py:16
  31.4 3.2 %collective-permute-done.8 = bf16[256,1024]{0,1:T(8,128)(2,1)S(1)} collective-permute-done((bf16[256,1024]{0,1:T(8,128)(2,1)S(1)}, bf16[256,1024]{0,1:T(8,128)(2,1)S(1)}, u32[]{:S(2)}, u32[]{:S(2)}) %collective-permute-start.8) | collective-permute-done | bytes 524320 | tf_op jit(solution)/shard_map/ppermute | solution.py:16
  34.6 2.1 %collective-permute-start.1 = (bf16[256,1024]{1,0:T(8,128)(2,1)S(1)}, bf16[256,1024]{1,0:T(8,128)(2,1)S(1)}, u32[]{:S(2)}, u32[]{:S(2)}) collective-permute-start(bf16[256,1024]{1,0:T(8,128)(2,1)S(1)} %copy-done), channel_id=1, source_target_pairs={{0,6},{2,8},{4,10},{6,12},{8,14},{10,16},{12,18},{14,20},{16,22},{... | collective-permute-start | bytes 1572872 | tf_op jit(solution)/shard_map/ppermute | solution.py:16
  36.8 7.3 %collective-permute-done.9 = bf16[256,1024]{0,1:T(8,128)(2,1)S(1)} collective-permute-done((bf16[256,1024]{0,1:T(8,128)(2,1)S(1)}, bf16[256,1024]{0,1:T(8,128)(2,1)S(1)}, u32[]{:S(2)}, u32[]{:S(2)}) %collective-permute-start.9) | collective-permute-done | bytes 524320 | tf_op jit(solution)/shard_map/ppermute | solution.py:16
  44.1 4.4 %collective-permute-start.2 = (bf16[256,1024]{1,0:T(8,128)(2,1)S(1)}, bf16[256,1024]{1,0:T(8,128)(2,1)S(1)}, u32[]{:S(2)}, u32[]{:S(2)}) collective-permute-start(bf16[256,1024]{1,0:T(8,128)(2,1)S(1)} %copy-done), channel_id=1, source_target_pairs={{0,4},{2,6},{4,8},{6,10},{8,12},{10,14},{12,16},{14,18},{16,20},{1... | collective-permute-start | bytes 1572872 | tf_op jit(solution)/shard_map/ppermute | solution.py:16
  48.6 7.7 %collective-permute-done.10 = bf16[256,1024]{0,1:T(8,128)(2,1)S(1)} collective-permute-done((bf16[256,1024]{0,1:T(8,128)(2,1)S(1)}, bf16[256,1024]{0,1:T(8,128)(2,1)S(1)}, u32[]{:S(2)}, u32[]{:S(2)}) %collective-permute-start.10) | collective-permute-done | bytes 524320 | tf_op jit(solution)/shard_map/ppermute | solution.py:16
  56.3 2.7 %collective-permute-start.3 = (bf16[256,1024]{1,0:T(8,128)(2,1)S(1)}, bf16[256,1024]{1,0:T(8,128)(2,1)S(1)}, u32[]{:S(2)}, u32[]{:S(2)}) collective-permute-start(bf16[256,1024]{1,0:T(8,128)(2,1)S(1)} %copy-done), channel_id=1, source_target_pairs={{0,2},{2,4},{4,6},{6,8},{8,10},{10,12},{12,14},{14,16},{16,18},{18... | collective-permute-start | bytes 1572872 | tf_op jit(solution)/shard_map/ppermute | solution.py:16
  59.1 9.5 %collective-permute-done.11 = bf16[256,1024]{0,1:T(8,128)(2,1)S(1)} collective-permute-done((bf16[256,1024]{0,1:T(8,128)(2,1)S(1)}, bf16[256,1024]{0,1:T(8,128)(2,1)S(1)}, u32[]{:S(2)}, u32[]{:S(2)}) %collective-permute-start.11) | collective-permute-done | bytes 524320 | tf_op jit(solution)/shard_map/ppermute | solution.py:16
  68.6 0.9 constant_dynamic-update-slice_fusion.4
  69.5 0.9 constant_dynamic-update-slice_fusion.3
  70.4 19.6 %collective-permute-done.2 = bf16[256,1024]{1,0:T(8,128)(2,1)S(1)} collective-permute-done((bf16[256,1024]{1,0:T(8,128)(2,1)S(1)}, bf16[256,1024]{1,0:T(8,128)(2,1)S(1)}, u32[]{:S(2)}, u32[]{:S(2)}) %collective-permute-start.2) | collective-permute-done | bytes 524320 | tf_op jit(solution)/shard_map/ppermute | solution.py:16
  90.0 0.8 constant_dynamic-update-slice_fusion.2
  90.8 10.9 %collective-permute-done.3 = bf16[256,1024]{1,0:T(8,128)(2,1)S(1)} collective-permute-done((bf16[256,1024]{1,0:T(8,128)(2,1)S(1)}, bf16[256,1024]{1,0:T(8,128)(2,1)S(1)}, u32[]{:S(2)}, u32[]{:S(2)}) %collective-permute-start.3) | collective-permute-done | bytes 524320 | tf_op jit(solution)/shard_map/ppermute | solution.py:16
  101.7 0.8 constant_dynamic-update-slice_fusion.1
  102.6 0.8 constant_dynamic-update-slice_fusion
  103.4 3.0 %copy.20 = bf16[1280,1024]{0,1:T(8,128)(2,1)S(1)} copy(bf16[1280,1024]{1,0:T(8,128)(2,1)} %constant_dynamic-update-slice_fusion) | data formatting | bytes 5242880 | tf_op jit(solution)/shard_map/concatenate | solution.py:62
  106.4 33.7 %while.11 = (s32[]{:T(128)}, bf16[8,256,2,128]{1,3,2,0:T(8,128)(2,1)}, bf16[8,1280,128]{1,2,0:T(8,128)(2,1)S(1)}, bf16[8,1280,128]{1,2,0:T(8,128)(2,1)}, bf16[8,...) while((s32[]{:T(128)}, ...), condition=%wide.region_3.4_spmd.clone, body=%wide.region_0.3_spmd.clone.sunk | while | flops 342227968 | bytes 9460829 | solution.py:47
  106.4 1.0 fusion.43
  107.5 1.6 %fusion.44 = (f32[2,256]{1,0:T(2,128)S(1)}, f32[2,256,1280]{1,2,0:T(8,128)S(1)}) fusion(bf16[8,256,2,128]{1,3,2,0:T(8,128)(2,1)} %get-tuple-element.168, s32[]{:T(128)} %get-tuple-element.155, bf16[8,1280,128]{1,2,0:T(8,128)(2,1)} %get-tuple-element.167, pred[256,1280]{0,1:T(8,128)(4,1)S(1)} %fusion.43), kind=kOutput, calls=%fused_computation.44.clone.1 | convolution fusion | flops 169737728 | bytes 3410944 | tf_op jit(solution)/shard_map/while/body/eval_jaxpr/tgd,sd->gts/dot_general | solution.py:36
  109.0 0.4 fusion.45
  109.4 1.2 fusion.46
  110.6 1.0 fusion.43
  111.7 1.6 %fusion.44 = (f32[2,256]{1,0:T(2,128)S(1)}, f32[2,256,1280]{1,2,0:T(8,128)S(1)}) fusion(bf16[8,256,2,128]{1,3,2,0:T(8,128)(2,1)} %get-tuple-element.168, s32[]{:T(128)} %get-tuple-element.155, bf16[8,1280,128]{1,2,0:T(8,128)(2,1)} %get-tuple-element.167, pred[256,1280]{0,1:T(8,128)(4,1)S(1)} %fusion.43), kind=kOutput, calls=%fused_computation.44.clone.1 | convolution fusion | flops 169737728 | bytes 3410944 | tf_op jit(solution)/shard_map/while/body/eval_jaxpr/tgd,sd->gts/dot_general | solution.py:36
  113.2 0.4 fusion.45
  113.6 1.3 fusion.46
  114.9 1.0 fusion.43
  115.9 1.6 %fusion.44 = (f32[2,256]{1,0:T(2,128)S(1)}, f32[2,256,1280]{1,2,0:T(8,128)S(1)}) fusion(bf16[8,256,2,128]{1,3,2,0:T(8,128)(2,1)} %get-tuple-element.168, s32[]{:T(128)} %get-tuple-element.155, bf16[8,1280,128]{1,2,0:T(8,128)(2,1)} %get-tuple-element.167, pred[256,1280]{0,1:T(8,128)(4,1)S(1)} %fusion.43), kind=kOutput, calls=%fused_computation.44.clone.1 | convolution fusion | flops 169737728 | bytes 3410944 | tf_op jit(solution)/shard_map/while/body/eval_jaxpr/tgd,sd->gts/dot_general | solution.py:36
  117.4 0.4 fusion.45
  117.8 1.3 fusion.46
  119.1 1.0 fusion.43
  120.1 1.6 %fusion.44 = (f32[2,256]{1,0:T(2,128)S(1)}, f32[2,256,1280]{1,2,0:T(8,128)S(1)}) fusion(bf16[8,256,2,128]{1,3,2,0:T(8,128)(2,1)} %get-tuple-element.168, s32[]{:T(128)} %get-tuple-element.155, bf16[8,1280,128]{1,2,0:T(8,128)(2,1)} %get-tuple-element.167, pred[256,1280]{0,1:T(8,128)(4,1)S(1)} %fusion.43), kind=kOutput, calls=%fused_computation.44.clone.1 | convolution fusion | flops 169737728 | bytes 3410944 | tf_op jit(solution)/shard_map/while/body/eval_jaxpr/tgd,sd->gts/dot_general | solution.py:36
  121.6 0.4 fusion.45
  122.0 1.3 fusion.46
  123.3 1.0 fusion.43
  124.3 1.6 %fusion.44 = (f32[2,256]{1,0:T(2,128)S(1)}, f32[2,256,1280]{1,2,0:T(8,128)S(1)}) fusion(bf16[8,256,2,128]{1,3,2,0:T(8,128)(2,1)} %get-tuple-element.168, s32[]{:T(128)} %get-tuple-element.155, bf16[8,1280,128]{1,2,0:T(8,128)(2,1)} %get-tuple-element.167, pred[256,1280]{0,1:T(8,128)(4,1)S(1)} %fusion.43), kind=kOutput, calls=%fused_computation.44.clone.1 | convolution fusion | flops 169737728 | bytes 3410944 | tf_op jit(solution)/shard_map/while/body/eval_jaxpr/tgd,sd->gts/dot_general | solution.py:36
  125.8 0.4 fusion.45
  126.2 1.3 fusion.46
  127.5 1.0 fusion.43
  128.5 1.6 %fusion.44 = (f32[2,256]{1,0:T(2,128)S(1)}, f32[2,256,1280]{1,2,0:T(8,128)S(1)}) fusion(bf16[8,256,2,128]{1,3,2,0:T(8,128)(2,1)} %get-tuple-element.168, s32[]{:T(128)} %get-tuple-element.155, bf16[8,1280,128]{1,2,0:T(8,128)(2,1)} %get-tuple-element.167, pred[256,1280]{0,1:T(8,128)(4,1)S(1)} %fusion.43), kind=kOutput, calls=%fused_computation.44.clone.1 | convolution fusion | flops 169737728 | bytes 3410944 | tf_op jit(solution)/shard_map/while/body/eval_jaxpr/tgd,sd->gts/dot_general | solution.py:36
  130.1 0.4 fusion.45
  130.4 1.3 fusion.46
  131.7 1.0 fusion.43
  132.7 1.6 %fusion.44 = (f32[2,256]{1,0:T(2,128)S(1)}, f32[2,256,1280]{1,2,0:T(8,128)S(1)}) fusion(bf16[8,256,2,128]{1,3,2,0:T(8,128)(2,1)} %get-tuple-element.168, s32[]{:T(128)} %get-tuple-element.155, bf16[8,1280,128]{1,2,0:T(8,128)(2,1)} %get-tuple-element.167, pred[256,1280]{0,1:T(8,128)(4,1)S(1)} %fusion.43), kind=kOutput, calls=%fused_computation.44.clone.1 | convolution fusion | flops 169737728 | bytes 3410944 | tf_op jit(solution)/shard_map/while/body/eval_jaxpr/tgd,sd->gts/dot_general | solution.py:36
  134.3 0.4 fusion.45
  134.6 1.3 fusion.46
  135.9 1.0 fusion.43
  136.9 1.6 %fusion.44 = (f32[2,256]{1,0:T(2,128)S(1)}, f32[2,256,1280]{1,2,0:T(8,128)S(1)}) fusion(bf16[8,256,2,128]{1,3,2,0:T(8,128)(2,1)} %get-tuple-element.168, s32[]{:T(128)} %get-tuple-element.155, bf16[8,1280,128]{1,2,0:T(8,128)(2,1)} %get-tuple-element.167, pred[256,1280]{0,1:T(8,128)(4,1)S(1)} %fusion.43), kind=kOutput, calls=%fused_computation.44.clone.1 | convolution fusion | flops 169737728 | bytes 3410944 | tf_op jit(solution)/shard_map/while/body/eval_jaxpr/tgd,sd->gts/dot_general | solution.py:36
  138.5 0.4 fusion.45
  138.8 1.3 fusion.46
  140.1 2.3 %copy.31 = bf16[256,2048]{1,0:T(8,128)(2,1)} copy(bf16[256,2048]{0,1:T(8,128)(2,1)} %bitcast.9) | data formatting | bytes 2097152 | tf_op jit(solution)/shard_map/reshape | solution.py:48
  (22 shorter events, 0.2 us)
Async XLA Ops:
  0.0 29.4 %copy-start = (bf16[256,1024]{1,0:T(8,128)(2,1)S(1)}, bf16[256,1024]{1,0:T(8,128)(2,1)}, u32[]{:S(2)}) copy-start(bf16[256,1024]{1,0:T(8,128)(2,1)} %param.8) | copy-start | bytes 1572868
  4.5 17.8 %collective-permute-start.4 = (s32[256]{0:T(256)S(1)}, s32[256]{0:T(256)S(1)}, u32[]{:S(2)}, u32[]{:S(2)}) collective-permute-start(s32[256]{0:T(256)S(1)} %broadcast_add_fusion.1), channel_id=1, source_target_pairs={{0,8},{2,10},{4,12},{6,14},{8,16},{10,18},{12,20},{14,22},{16,24},... | collective-permute-start | bytes 3080 | tf_op jit(solution)/shard_map/ppermute | solution.py:16
  8.0 17.4 %collective-permute-start.5 = (s32[256]{0:T(256)S(1)}, s32[256]{0:T(256)S(1)}, u32[]{:S(2)}, u32[]{:S(2)}) collective-permute-start(s32[256]{0:T(256)S(1)} %broadcast_add_fusion.1), channel_id=1, source_target_pairs={{0,6},{2,8},{4,10},{6,12},{8,14},{10,16},{12,18},{14,20},{16,22},{... | collective-permute-start | bytes 3080 | tf_op jit(solution)/shard_map/ppermute | solution.py:16
  9.9 17.5 %collective-permute-start.6 = (s32[256]{0:T(256)S(1)}, s32[256]{0:T(256)S(1)}, u32[]{:S(2)}, u32[]{:S(2)}) collective-permute-start(s32[256]{0:T(256)S(1)} %broadcast_add_fusion.1), channel_id=1, source_target_pairs={{0,4},{2,6},{4,8},{6,10},{8,12},{10,14},{12,16},{14,18},{16,20},{1... | collective-permute-start | bytes 3080 | tf_op jit(solution)/shard_map/ppermute | solution.py:16
  13.3 16.1 %collective-permute-start.7 = (s32[256]{0:T(256)S(1)}, s32[256]{0:T(256)S(1)}, u32[]{:S(2)}, u32[]{:S(2)}) collective-permute-start(s32[256]{0:T(256)S(1)} %broadcast_add_fusion.1), channel_id=1, source_target_pairs={{0,2},{2,4},{4,6},{6,8},{8,10},{10,12},{12,14},{14,16},{16,18},{18... | collective-permute-start | bytes 3080 | tf_op jit(solution)/shard_map/ppermute | solution.py:16
  17.9 16.7 %collective-permute-start.8 = (bf16[256,1024]{0,1:T(8,128)(2,1)S(1)}, bf16[256,1024]{0,1:T(8,128)(2,1)S(1)}, u32[]{:S(2)}, u32[]{:S(2)}) collective-permute-start(bf16[256,1024]{0,1:T(8,128)(2,1)S(1)} %copy.21), channel_id=1, source_target_pairs={{0,8},{2,10},{4,12},{6,14},{8,16},{10,18},{12,20},{14,22},{16,24},... | collective-permute-start | bytes 1572872 | tf_op jit(solution)/shard_map/ppermute | solution.py:16
  22.3 21.8 %collective-permute-start.9 = (bf16[256,1024]{0,1:T(8,128)(2,1)S(1)}, bf16[256,1024]{0,1:T(8,128)(2,1)S(1)}, u32[]{:S(2)}, u32[]{:S(2)}) collective-permute-start(bf16[256,1024]{0,1:T(8,128)(2,1)S(1)} %copy.21), channel_id=1, source_target_pairs={{0,6},{2,8},{4,10},{6,12},{8,14},{10,16},{12,18},{14,20},{16,22},{... | collective-permute-start | bytes 1572872 | tf_op jit(solution)/shard_map/ppermute | solution.py:16
  25.4 30.9 %collective-permute-start.10 = (bf16[256,1024]{0,1:T(8,128)(2,1)S(1)}, bf16[256,1024]{0,1:T(8,128)(2,1)S(1)}, u32[]{:S(2)}, u32[]{:S(2)}) collective-permute-start(bf16[256,1024]{0,1:T(8,128)(2,1)S(1)} %copy.21), channel_id=1, source_target_pairs={{0,4},{2,6},{4,8},{6,10},{8,12},{10,14},{12,16},{14,18},{16,20},{1... | collective-permute-start | bytes 1572872 | tf_op jit(solution)/shard_map/ppermute | solution.py:16
  27.4 41.1 %collective-permute-start.11 = (bf16[256,1024]{0,1:T(8,128)(2,1)S(1)}, bf16[256,1024]{0,1:T(8,128)(2,1)S(1)}, u32[]{:S(2)}, u32[]{:S(2)}) collective-permute-start(bf16[256,1024]{0,1:T(8,128)(2,1)S(1)} %copy.21), channel_id=1, source_target_pairs={{0,2},{2,4},{4,6},{6,8},{8,10},{10,12},{12,14},{14,16},{16,18},{18... | collective-permute-start | bytes 1572872 | tf_op jit(solution)/shard_map/ppermute | solution.py:16
  29.4 39.2 %collective-permute-start = (bf16[256,1024]{1,0:T(8,128)(2,1)S(1)}, bf16[256,1024]{1,0:T(8,128)(2,1)S(1)}, u32[]{:S(2)}, u32[]{:S(2)}) collective-permute-start(bf16[256,1024]{1,0:T(8,128)(2,1)S(1)} %copy-done), channel_id=1, source_target_pairs={{0,8},{2,10},{4,12},{6,14},{8,16},{10,18},{12,20},{14,22},{16,24},... | collective-permute-start | bytes 1572872 | tf_op jit(solution)/shard_map/ppermute | solution.py:16
  34.6 34.9 %collective-permute-start.1 = (bf16[256,1024]{1,0:T(8,128)(2,1)S(1)}, bf16[256,1024]{1,0:T(8,128)(2,1)S(1)}, u32[]{:S(2)}, u32[]{:S(2)}) collective-permute-start(bf16[256,1024]{1,0:T(8,128)(2,1)S(1)} %copy-done), channel_id=1, source_target_pairs={{0,6},{2,8},{4,10},{6,12},{8,14},{10,16},{12,18},{14,20},{16,22},{... | collective-permute-start | bytes 1572872 | tf_op jit(solution)/shard_map/ppermute | solution.py:16
  44.1 45.9 %collective-permute-start.2 = (bf16[256,1024]{1,0:T(8,128)(2,1)S(1)}, bf16[256,1024]{1,0:T(8,128)(2,1)S(1)}, u32[]{:S(2)}, u32[]{:S(2)}) collective-permute-start(bf16[256,1024]{1,0:T(8,128)(2,1)S(1)} %copy-done), channel_id=1, source_target_pairs={{0,4},{2,6},{4,8},{6,10},{8,12},{10,14},{12,16},{14,18},{16,20},{1... | collective-permute-start | bytes 1572872 | tf_op jit(solution)/shard_map/ppermute | solution.py:16
  56.3 45.4 %collective-permute-start.3 = (bf16[256,1024]{1,0:T(8,128)(2,1)S(1)}, bf16[256,1024]{1,0:T(8,128)(2,1)S(1)}, u32[]{:S(2)}, u32[]{:S(2)}) collective-permute-start(bf16[256,1024]{1,0:T(8,128)(2,1)S(1)} %copy-done), channel_id=1, source_target_pairs={{0,2},{2,4},{4,6},{6,8},{8,10},{10,12},{12,14},{14,16},{16,18},{18... | collective-permute-start | bytes 1572872 | tf_op jit(solution)/shard_map/ppermute | solution.py:16
  68.6 34.0 %copy-start.1 = (bf16[1280,1024]{0,1:T(8,128)(2,1)}, bf16[1280,1024]{0,1:T(8,128)(2,1)S(1)}, u32[]{:S(2)}) copy-start(bf16[1280,1024]{0,1:T(8,128)(2,1)S(1)} %constant_dynamic-update-slice_fusion.5) | copy-start | bytes 7864324
where the time goes:
time: 143 us; the launch traced here: 142 us
  waiting for transfers between devices  58.2 us (41%)
  starting transfers between devices  32.4 us (23%)
  matrix products  22.6 us (16%)
  local copies, waits for them, and re-layouts  13.2 us (9%)
  other arithmetic  11 us (8%)
  blocking collectives  4.49 us (3%)
    ppermute x12, waiting for transfers between devices, from_behind(): lax.ppermute(value, axis, [(source, source + steps) for source in range(i...  58.2 us
    ppermute x12, starting transfers between devices, from_behind(): lax.ppermute(value, axis, [(source, source + steps) for source in range(i...  32.4 us
    dot_general x8, matrix products, one_head(): jnp.einsum('tgd,sd->gts', head_q, head_k, preferred_element_type=jnp.floa...  12.4 us
    dot_general x8, matrix products, one_head(): jnp.einsum('gts,sd->tgd', rounded, head_v, preferred_element_type=jnp.flo...  10.1 us
    and x8, other arithmetic, attend(): (key_ids[None, :] == query_ids[:, None]) & (key_pos[None, :] <= query_pos...  8.07 us
    unnamed x18, local copies, waits for them, and re-layouts  7.11 us
    all_gather x1, blocking collectives, body(): own_ids = lax.all_gather(segment_ids, 'head', axis=0, tiled=True)  4.49 us
    concatenate x2, local copies, waits for them, and re-layouts, body(): all_values = jnp.concatenate([piece[1] for piece in ordered], axis=0)  3.81 us
  transfers between devices with their start and end apart: 12, of which 6 were waited for; matrix products, arithmetic and copies ran while one was open for 4% of the time, Pallas kernels for 0%

commit v1 on v0

v1 whole, which is shorter than its diff:
```python
import functools
import math

import jax
import jax.numpy as jnp
from jax import lax
from jax.experimental import pallas as pl
from jax.experimental.pallas import tpu as pltpu
from jax.sharding import PartitionSpec as P

HEAD_WIDTH = 128
WINDOW = 1024
HIDDEN = -1e30
EXPONENT_SCALE = 168.0 ** (-0.5) * math.log2(math.e)


def weights_kernel(q_ref, k0, k1, k2, k3, k4, i0, i1, i2, i3, i4, p_ref, total_ref, bias):
    tok_rows = k0.shape[0]
    group = q_ref.shape[1] // HEAD_WIDTH

    @pl.when(pl.program_id(0) == 0)
    def _():
        own = jnp.broadcast_to(i0[...], (tok_rows, tok_rows)).T
        row = lax.broadcasted_iota(jnp.int32, (tok_rows, tok_rows), 0)
        col = lax.broadcasted_iota(jnp.int32, (tok_rows, tok_rows), 1)
        for b, ids in enumerate((i0, i1, i2, i3, i4)):
            seen = ids[...] == own
            if b == 0:
                seen = seen & (col <= row)
            if b == 1:
                seen = seen & (col > row)
            bias[b] = jnp.where(seen, 0.0, HIDDEN)

    q = jnp.concatenate([q_ref[:, g * HEAD_WIDTH:(g + 1) * HEAD_WIDTH] for g in range(group)], axis=0)
    scores = []
    for b, k in enumerate((k0, k1, k2, k3, k4)):
        s = lax.dot_general(q, k[...], (((1,), (1,)), ((), ())), preferred_element_type=jnp.float32)
        s = s.reshape(group, tok_rows, tok_rows) * EXPONENT_SCALE + bias[b][None]
        scores.append(s.reshape(group * tok_rows, tok_rows))
    top = functools.reduce(jnp.maximum, scores)
    top = jnp.max(top, axis=1, keepdims=True)
    sums = None
    for b, s in enumerate(scores):
        w = jnp.exp2(s - top)
        sums = w if sums is None else sums + w
        p_ref[0, :, b * tok_rows:(b + 1) * tok_rows] = w.astype(jnp.bfloat16)
    total = jnp.sum(sums, axis=1, keepdims=True)
    total_ref[0] = jnp.broadcast_to(total, (group * tok_rows, HEAD_WIDTH))


def weights(queries, blocks, ids):
    tok_rows = queries.shape[0]
    kv_heads = blocks[0].shape[1] // HEAD_WIDTH
    group = queries.shape[1] // blocks[0].shape[1]
    span = len(blocks) * tok_rows
    k_spec = pl.BlockSpec((tok_rows, HEAD_WIDTH), lambda h: (0, h))
    i_spec = pl.BlockSpec((1, tok_rows), lambda h: (0, 0))
    return pl.pallas_call(
        weights_kernel,
        grid=(kv_heads,),
        in_specs=[pl.BlockSpec((tok_rows, group * HEAD_WIDTH), lambda h: (0, h))] + [k_spec] * 5 + [i_spec] * 5,
        out_specs=[
            pl.BlockSpec((1, group * tok_rows, span), lambda h: (h, 0, 0)),
            pl.BlockSpec((1, group * tok_rows, HEAD_WIDTH), lambda h: (h, 0, 0)),
        ],
        out_shape=[
            jax.ShapeDtypeStruct((kv_heads, group * tok_rows, span), jnp.bfloat16),
            jax.ShapeDtypeStruct((kv_heads, group * tok_rows, HEAD_WIDTH), jnp.float32),
        ],
        scratch_shapes=[pltpu.VMEM((5, tok_rows, tok_rows), jnp.float32)],
        cost_estimate=pl.CostEstimate(
            flops=2 * queries.size * span, transcendentals=queries.size // HEAD_WIDTH * span, bytes_accessed=queries.size * 2),
        name="weights",
    )(queries, *blocks, *ids)


def first_kernel(p_ref, v0, v1, v2, acc_ref):
    tok_rows = v0.shape[0]
    acc = None
    for b, v in enumerate((v0, v1, v2)):
        d = jnp.dot(p_ref[0, :, b * tok_rows:(b + 1) * tok_rows], v[...], preferred_element_type=jnp.float32)
        acc = d if acc is None else acc + d
    acc_ref[0] = acc


def first(p, blocks):
    kv_heads, rows, span = p.shape
    tok_rows = blocks[0].shape[0]
    v_spec = pl.BlockSpec((tok_rows, HEAD_WIDTH), lambda h: (0, h))
    return pl.pallas_call(
        first_kernel,
        grid=(kv_heads,),
        in_specs=[pl.BlockSpec((1, rows, 3 * tok_rows), lambda h: (h, 0, 0))] + [v_spec] * 3,
        out_specs=pl.BlockSpec((1, rows, HEAD_WIDTH), lambda h: (h, 0, 0)),
        out_shape=jax.ShapeDtypeStruct((kv_heads, rows, HEAD_WIDTH), jnp.float32),
        cost_estimate=pl.CostEstimate(flops=2 * kv_heads * rows * 3 * tok_rows * HEAD_WIDTH, transcendentals=0, bytes_accessed=p.size),
        name="first",
    )(p, *blocks)


def last_kernel(p3, p4, v3, v4, acc_ref, total_ref, out_ref):
    tok_rows = v3.shape[0]
    group = out_ref.shape[1] // HEAD_WIDTH
    acc = acc_ref[0]
    acc = acc + jnp.dot(p3[0], v3[...], preferred_element_type=jnp.float32)
    acc = acc + jnp.dot(p4[0], v4[...], preferred_element_type=jnp.float32)
    out = (acc / total_ref[0]).astype(out_ref.dtype)
    for g in range(group):
        out_ref[:, g * HEAD_WIDTH:(g + 1) * HEAD_WIDTH] = out[g * tok_rows:(g + 1) * tok_rows]


def last(p, blocks, acc, total):
    kv_heads, rows, span = p.shape
    tok_rows = blocks[0].shape[0]
    group = rows // tok_rows
    v_spec = pl.BlockSpec((tok_rows, HEAD_WIDTH), lambda h: (0, h))
    a_spec = pl.BlockSpec((1, rows, HEAD_WIDTH), lambda h: (h, 0, 0))
    return pl.pallas_call(
        last_kernel,
        grid=(kv_heads,),
        in_specs=[
            pl.BlockSpec((1, rows, tok_rows), lambda h: (h, 0, 3)),
            pl.BlockSpec((1, rows, tok_rows), lambda h: (h, 0, 4)),
            v_spec, v_spec, a_spec, a_spec],
        out_specs=pl.BlockSpec((tok_rows, group * HEAD_WIDTH), lambda h: (0, h)),
        out_shape=jax.ShapeDtypeStruct((tok_rows, kv_heads * group * HEAD_WIDTH), jnp.bfloat16),
        cost_estimate=pl.CostEstimate(flops=2 * kv_heads * rows * 2 * tok_rows * HEAD_WIDTH, transcendentals=0, bytes_accessed=p.size),
        name="last",
    )(p, p, *blocks, acc, total)


def body(queries, keys, values, segment_ids):
    tok_rows = keys.shape[0]
    reach = WINDOW // tok_rows
    count = lax.axis_size("seq")
    assert reach == 4 and reach * tok_rows == WINDOW and count % reach == 0
    place = lax.axis_index("seq") % reach
    ahead = [(i, i + reach) for i in range(count - reach)]
    across = [(i, i ^ 2) for i in range(count)]
    beside = [(i, i ^ 1) for i in range(count)]

    def send(x, pairs):
        return lax.ppermute(x, "seq", pairs)

    key_far = send(keys, ahead)
    value_far = send(values, ahead)
    own_ids = lax.all_gather(segment_ids, "head", axis=0, tiled=True) + 1
    id_far = send(own_ids, ahead)

    def spread(own, far):
        two = send(jnp.where(place >= 2, far, own), across)
        one = send(jnp.where(place % 2 == 1, far, own), beside)
        three = send(two, beside)
        return own, far, one, two, three

    ids = [x[None] for x in spread(own_ids, id_far)]
    ks = spread(keys, key_far)
    p, total = weights(queries, ks, ids)
    vs = spread(values, value_far)
    acc = first(p, vs[:3])
    return last(p, vs[3:], acc, total)


def solution(mesh):
    in_specs = (P("seq", "head"), P("seq", "head"), P("seq", "head"), P(("seq", "head")))
    out_specs = P("seq", "head")
    return jax.shard_map(body, mesh=mesh, in_specs=in_specs, out_specs=out_specs, check_vma=False)
```

time: 143 us -> 85.8 us (0.60)
  Pallas kernels: 0 us -> 27.7 us
  waiting for transfers between devices: 58.2 us -> 31.5 us
  matrix products: 22.6 us -> 0 us
  starting transfers between devices: 32.4 us -> 15.4 us
  local copies, waits for them, and re-layouts: 13.2 us -> 3.19 us
  other arithmetic: 11 us -> 1.95 us
    pallas_call x0 -> x3, Pallas kernels: none -> 27.7 us  [the longest x1 11.9 us: weights(): pl.pallas_call(weights_kernel, grid=(kv_heads,), in_specs=[pl.BlockSpec((...]
    ppermute x12, waiting for transfers between devices: 58.2 us -> 31.5 us  [send(): return lax.ppermute(x, 'seq', pairs)]
    dot_general x16 -> x0, matrix products: 22.6 us -> none  [the longest x8 12.4 us: one_head(): jnp.einsum('tgd,sd->gts', head_q, head_k, preferred_element_type=jnp.floa...]
    ppermute x12, starting transfers between devices: 32.4 us -> 15.4 us  [send(): return lax.ppermute(x, 'seq', pairs)]
    and x8 -> x0, other arithmetic: 8.07 us -> none  [attend(): (key_ids[None, :] == query_ids[:, None]) & (key_pos[None, :] <= query_pos...]
    unnamed x18 -> x28, local copies, waits for them, and re-layouts: 7.11 us -> 3.19 us
    concatenate x3 -> x0, local copies, waits for them, and re-layouts: 3.84 us -> none  [the longest x2 3.81 us: body(): all_values = jnp.concatenate([piece[1] for piece in ordered], axis=0)]
    reduce_sum x8 -> x0, other arithmetic: 2.93 us -> none  [one_head(): total = jnp.sum(weights, axis=2)]
  transfers between devices with their start and end apart: 12 -> 12, of which waited for: 6 -> 8; matrix products, arithmetic and copies ran while one was open for 4% -> 2% of each run, Pallas kernels for 0% -> 24%
where the time goes in v1:
time: 85.8 us; the launch traced here: 84.2 us
  waiting for transfers between devices  31.5 us (37%)
  Pallas kernels  27.7 us (32%)
  starting transfers between devices  15.4 us (18%)
  blocking collectives  4.24 us (5%)
  local copies, waits for them, and re-layouts  3.19 us (4%)
  other arithmetic  1.95 us (2%)
    ppermute x12, waiting for transfers between devices, send(): return lax.ppermute(x, 'seq', pairs)  31.5 us
    ppermute x12, starting transfers between devices, send(): return lax.ppermute(x, 'seq', pairs)  15.4 us
    pallas_call x1, Pallas kernels, weights(): pl.pallas_call(weights_kernel, grid=(kv_heads,), in_specs=[pl.BlockSpec((...  11.9 us
    pallas_call x1, Pallas kernels, first(): pl.pallas_call(first_kernel, grid=(kv_heads,), in_specs=[pl.BlockSpec((1,...  8.01 us
    pallas_call x1, Pallas kernels, last(): pl.pallas_call(last_kernel, grid=(kv_heads,), in_specs=[pl.BlockSpec((1,...  7.85 us
    all_gather x1, blocking collectives, body(): own_ids = lax.all_gather(segment_ids, 'head', axis=0, tiled=True) + 1  4.24 us
    unnamed x28, local copies, waits for them, and re-layouts  3.19 us
  transfers between devices with their start and end apart: 12, of which 8 were waited for; matrix products, arithmetic and copies ran while one was open for 2% of the time, Pallas kernels for 24%

profile of v1, /device:TPU:10, one launch (start us, length us, event | category | flops | bytes accessed | tf_op | source)
XLA Modules:
  0.0 84.2 jit_solution(6514868451559839175)
XLA Ops:
  0.0 0.0 copy-start
  0.0 3.6 %collective-permute-start = (bf16[256,1024]{1,0:T(8,128)(2,1)}, bf16[256,1024]{1,0:T(8,128)(2,1)S(1)}, u32[]{:S(2)}, u32[]{:S(2)}) collective-permute-start(bf16[256,1024]{1,0:T(8,128)(2,1)} %k0.1), channel_id=1, source_target_pairs={{0,8},{2,10},{4,12},{6,14},{8,16},{10,18},{12,20},{14,22},{16,24},... | collective-permute-start | bytes 1572872 | tf_op jit(solution)/shard_map/ppermute | solution.py:143
  3.6 3.5 %collective-permute-start.8 = (bf16[256,1024]{1,0:T(8,128)(2,1)}, bf16[256,1024]{1,0:T(8,128)(2,1)S(1)}, u32[]{:S(2)}, u32[]{:S(2)}) collective-permute-start(bf16[256,1024]{1,0:T(8,128)(2,1)} %v0.1), channel_id=1, source_target_pairs={{0,8},{2,10},{4,12},{6,14},{8,16},{10,18},{12,20},{14,22},{16,24},... | collective-permute-start | bytes 1572872 | tf_op jit(solution)/shard_map/ppermute | solution.py:143
  7.1 0.0 copy-start.13
  7.2 9.9 %collective-permute-done.k1 = bf16[256,1024]{1,0:T(8,128)(2,1)S(1)} collective-permute-done((bf16[256,1024]{1,0:T(8,128)(2,1)}, bf16[256,1024]{1,0:T(8,128)(2,1)S(1)}, u32[]{:S(2)}, u32[]{:S(2)}) %collective-permute-start) | collective-permute-done | bytes 524320 | tf_op jit(solution)/shard_map/ppermute | solution.py:143
  17.0 0.0 copy-start.3
  17.0 1.3 %broadcast_select_fusion.1 = (bf16[256,1024]{1,0:T(8,128)(2,1)S(1)}, bf16[256,1024]{1,0:T(8,128)(2,1)S(1)}) fusion(bf16[256,1024]{1,0:T(8,128)(2,1)S(1)} %collective-permute-done.k1, bf16[256,1024]{1,0:T(8,128)(2,1)} %k0.1, pred[]{:T(512)S(6)} %ge.2, pred[]{:T(512)S(6)} %eq.10), kind=kLoop, calls=%fused_computation.1 | loop fusion | flops 524288 | bytes 2097154 | tf_op jit(solution)/shard_map/jit(_where)/select_n | solution.py:151
  18.3 1.6 %collective-permute-start.2 = (bf16[256,1024]{1,0:T(8,128)(2,1)S(1)}, bf16[256,1024]{1,0:T(8,128)(2,1)S(1)}, u32[]{:S(2)}, u32[]{:S(2)}) collective-permute-start(bf16[256,1024]{1,0:T(8,128)(2,1)S(1)} %get-tuple-element.11), channel_id=1, source_target_pairs={{0,4},{2,6},{4,0},{6,2},{8,12},{10,14},{12,8},{14,10},{16,20},{18,... | collective-permute-start | bytes 1572872 | tf_op jit(solution)/shard_map/ppermute | solution.py:143
  19.9 7.2 %collective-permute-done.8.v1 = bf16[256,1024]{1,0:T(8,128)(2,1)S(1)} collective-permute-done((bf16[256,1024]{1,0:T(8,128)(2,1)}, bf16[256,1024]{1,0:T(8,128)(2,1)S(1)}, u32[]{:S(2)}, u32[]{:S(2)}) %collective-permute-start.8) | collective-permute-done | bytes 524320 | tf_op jit(solution)/shard_map/ppermute | solution.py:143
  27.1 0.0 copy-done
  27.1 0.0 copy-start.1
  27.1 0.1 broadcast_select_fusion.2
  27.2 0.0 copy-done.3
  27.2 1.6 %collective-permute-start.9 = (bf16[256,1024]{1,0:T(8,128)(2,1)S(1)}, bf16[256,1024]{1,0:T(8,128)(2,1)S(1)}, u32[]{:S(2)}, u32[]{:S(2)}) collective-permute-start(bf16[256,1024]{1,0:T(8,128)(2,1)S(1)} %get-tuple-element.10), channel_id=1, source_target_pairs={{0,4},{2,6},{4,0},{6,2},{8,12},{10,14},{12,8},{14,10},{16,20},{18,... | collective-permute-start | bytes 1572872 | tf_op jit(solution)/shard_map/ppermute | solution.py:143
  28.8 0.0 collective-permute-start.1
  28.8 2.5 %collective-permute-done.2.k3 = bf16[256,1024]{1,0:T(8,128)(2,1)S(1)} collective-permute-done((bf16[256,1024]{1,0:T(8,128)(2,1)S(1)}, bf16[256,1024]{1,0:T(8,128)(2,1)S(1)}, u32[]{:S(2)}, u32[]{:S(2)}) %collective-permute-start.2) | collective-permute-done | bytes 524320 | tf_op jit(solution)/shard_map/ppermute | solution.py:143
  31.3 0.0 copy-start.7
  31.3 0.0 collective-permute-start.3
  31.3 0.0 copy-done.13
  31.3 4.2 %all-gather = s32[2,1,128]{2,1,0:T(1,128)S(1)} all-gather(s32[1,1,128]{2,1,0:T(1,128)S(1)} %bitcast.14), channel_id=1, replica_groups=mesh['seq'=16,'head'=2] {'head'}, dimensions={0}, use_global_device_ids=true | all-gather | bytes 1536 | tf_op jit(solution)/shard_map/all_gather | solution.py:147
  35.5 0.0 collective-permute-start.11
  35.5 5.8 %collective-permute-done.9.v3 = bf16[256,1024]{1,0:T(8,128)(2,1)S(1)} collective-permute-done((bf16[256,1024]{1,0:T(8,128)(2,1)S(1)}, bf16[256,1024]{1,0:T(8,128)(2,1)S(1)}, u32[]{:S(2)}, u32[]{:S(2)}) %collective-permute-start.9) | collective-permute-done | bytes 524320 | tf_op jit(solution)/shard_map/ppermute | solution.py:143
  41.3 0.0 copy-start.4
  41.3 0.0 collective-permute-start.10
  41.3 0.6 broadcast_add_fusion
  41.9 3.5 %collective-permute-start.4 = (s32[256]{0:T(256)S(1)}, s32[256]{0:T(256)S(1)}, u32[]{:S(2)}, u32[]{:S(2)}) collective-permute-start(s32[256]{0:T(256)S(1)} %bitcast.8), channel_id=1, source_target_pairs={{0,8},{2,10},{4,12},{6,14},{8,16},{10,18},{12,20},{14,22},{16,24},... | collective-permute-start | bytes 3080 | tf_op jit(solution)/shard_map/ppermute | solution.py:143
  45.4 2.0 %collective-permute-done.4 = s32[256]{0:T(256)S(1)} collective-permute-done((s32[256]{0:T(256)S(1)}, s32[256]{0:T(256)S(1)}, u32[]{:S(2)}, u32[]{:S(2)}) %collective-permute-start.4) | collective-permute-done | bytes 1056 | tf_op jit(solution)/shard_map/ppermute | solution.py:143
  47.3 0.0 copy-start.6
  47.3 1.5 %collective-permute-start.6 = (s32[256]{0:T(256)S(1)}, s32[256]{0:T(256)S(1)}, u32[]{:S(2)}, u32[]{:S(2)}) collective-permute-start(s32[256]{0:T(256)S(1)} %get-tuple-element.13), channel_id=1, source_target_pairs={{0,4},{2,6},{4,0},{6,2},{8,12},{10,14},{12,8},{14,10},{16,20},{18,... | collective-permute-start | bytes 3080 | tf_op jit(solution)/shard_map/ppermute | solution.py:143
  48.9 2.1 %collective-permute-done.6 = s32[256]{0:T(256)S(1)} collective-permute-done((s32[256]{0:T(256)S(1)}, s32[256]{0:T(256)S(1)}, u32[]{:S(2)}, u32[]{:S(2)}) %collective-permute-start.6) | collective-permute-done | bytes 1056 | tf_op jit(solution)/shard_map/ppermute | solution.py:143
  50.9 0.0 copy-start.10
  50.9 0.0 collective-permute-start.5
  50.9 1.2 %collective-permute-done.5 = s32[256]{0:T(256)S(1)} collective-permute-done((s32[256]{0:T(256)S(1)}, s32[256]{0:T(256)S(1)}, u32[]{:S(2)}, u32[]{:S(2)}) %collective-permute-start.5) | collective-permute-done | bytes 1056 | tf_op jit(solution)/shard_map/ppermute | solution.py:143
  52.1 0.0 copy-start.11
  52.1 0.2 collective-permute-start.7
  52.3 1.0 %collective-permute-done.7 = s32[256]{0:T(256)S(1)} collective-permute-done((s32[256]{0:T(256)S(1)}, s32[256]{0:T(256)S(1)}, u32[]{:S(2)}, u32[]{:S(2)}) %collective-permute-start.7) | collective-permute-done | bytes 1056 | tf_op jit(solution)/shard_map/ppermute | solution.py:143
  53.2 0.0 copy-start.12
  53.3 0.0 collective-permute-done.1.k2
  53.3 0.0 copy-start.8
  53.3 0.0 collective-permute-done.3.k4
  53.3 0.8 copy-done.8
  54.0 0.0 copy-start.9
  54.0 0.8 copy-done.9
  54.8 0.0 copy-done.7
  54.8 0.0 copy-done.6
  54.8 0.0 copy-done.10
  54.8 0.0 copy-done.11
  54.9 0.0 copy-done.12
  54.9 11.9 %weights.1 = (bf16[8,512,1280]{2,1,0:T(8,128)(2,1)}, f32[8,512,128]{2,1,0:T(8,128)}) custom-call(bf16[256,2048]{1,0:T(8,128)(2,1)} %q_ref.1, bf16[256,1024]{1,0:T(8,128)(2,1)} %k0.1, bf16[256,1024]{1,0:T(8,128)(2,1)} %copy-done.3, bf16[256,1024]{1,0:T(8,128)(2,1)} %copy-done.8, bf16[256,1024]{1,0:T(8,128)(2,1)} %copy-done.7, bf16[256,1024]{1,0:T(8,128)(2,1)} %copy-done.9, ...), custom_call_target="tpu_custom_call" | custom-call | flops 1342177280 | bytes 1048576 | tf_op jit(solution)/shard_map/weights/pallas_call | solution.py:58
  66.7 0.0 copy-done.1
  66.7 0.0 copy-done.4
  66.7 0.0 collective-permute-done.11.v2
  66.8 0.0 copy-start.2
  66.8 0.8 copy-done.2
  67.6 8.0 %first.1.acc_ref = f32[8,512,128]{2,1,0:T(8,128)} custom-call(bf16[8,512,1280]{2,1,0:T(8,128)(2,1)} %get-tuple-element.7.p_ref.p3.p4, bf16[256,1024]{1,0:T(8,128)(2,1)} %v0.1, bf16[256,1024]{1,0:T(8,128)(2,1)} %copy-done.1, bf16[256,1024]{1,0:T(8,128)(2,1)} %copy-done.2), custom_call_target="tpu_custom_call" | custom-call | flops 805306368 | bytes 5242880 | tf_op jit(solution)/shard_map/first/pallas_call | solution.py:90
  75.6 0.0 collective-permute-done.10.v4
  75.6 0.0 copy-start.5
  75.6 0.8 copy-done.5
  76.4 7.8 %last.1 = bf16[256,2048]{1,0:T(8,128)(2,1)} custom-call(bf16[8,512,1280]{2,1,0:T(8,128)(2,1)} %get-tuple-element.7.p_ref.p3.p4, bf16[8,512,1280]{2,1,0:T(8,128)(2,1)} %get-tuple-element.7.p_ref.p3.p4, bf16[256,1024]{1,0:T(8,128)(2,1)} %copy-done.4, bf16[256,1024]{1,0:T(8,128)(2,1)} %copy-done.5, f32[8,512,128]{2,1,0:T(8,128)} %first.1.acc_ref, ...), custom_call_target="tpu_custom_call" | custom-call | flops 536870912 | bytes 5242880 | tf_op jit(solution)/shard_map/last/pallas_call | solution.py:118
  (1 shorter events, 0.0 us)
Async XLA Ops:
  0.0 27.1 %copy-start = (bf16[256,1024]{1,0:T(8,128)(2,1)S(1)}, bf16[256,1024]{1,0:T(8,128)(2,1)}, u32[]{:S(2)}) copy-start(bf16[256,1024]{1,0:T(8,128)(2,1)} %v0.1) | copy-start | bytes 1572868
  0.0 17.0 %collective-permute-start = (bf16[256,1024]{1,0:T(8,128)(2,1)}, bf16[256,1024]{1,0:T(8,128)(2,1)S(1)}, u32[]{:S(2)}, u32[]{:S(2)}) collective-permute-start(bf16[256,1024]{1,0:T(8,128)(2,1)} %k0.1), channel_id=1, source_target_pairs={{0,8},{2,10},{4,12},{6,14},{8,16},{10,18},{12,20},{14,22},{16,24},... | collective-permute-start | bytes 1572872 | tf_op jit(solution)/shard_map/ppermute | solution.py:143
  3.6 23.5 %collective-permute-start.8 = (bf16[256,1024]{1,0:T(8,128)(2,1)}, bf16[256,1024]{1,0:T(8,128)(2,1)S(1)}, u32[]{:S(2)}, u32[]{:S(2)}) collective-permute-start(bf16[256,1024]{1,0:T(8,128)(2,1)} %v0.1), channel_id=1, source_target_pairs={{0,8},{2,10},{4,12},{6,14},{8,16},{10,18},{12,20},{14,22},{16,24},... | collective-permute-start | bytes 1572872 | tf_op jit(solution)/shard_map/ppermute | solution.py:143
  7.1 24.2 %copy-start.13 = (s32[128]{0:T(128)S(1)}, s32[128]{0:T(128)}, u32[]{:S(2)}) copy-start(s32[128]{0:T(128)} %param.7) | copy-start | bytes 1540
  17.0 10.2 %copy-start.3 = (bf16[256,1024]{1,0:T(8,128)(2,1)}, bf16[256,1024]{1,0:T(8,128)(2,1)S(1)}, u32[]{:S(2)}) copy-start(bf16[256,1024]{1,0:T(8,128)(2,1)S(1)} %collective-permute-done.k1) | copy-start | bytes 1572868
  18.3 13.0 %collective-permute-start.2 = (bf16[256,1024]{1,0:T(8,128)(2,1)S(1)}, bf16[256,1024]{1,0:T(8,128)(2,1)S(1)}, u32[]{:S(2)}, u32[]{:S(2)}) collective-permute-start(bf16[256,1024]{1,0:T(8,128)(2,1)S(1)} %get-tuple-element.11), channel_id=1, source_target_pairs={{0,4},{2,6},{4,0},{6,2},{8,12},{10,14},{12,8},{14,10},{16,20},{18,... | collective-permute-start | bytes 1572872 | tf_op jit(solution)/shard_map/ppermute | solution.py:143
  27.1 39.6 %copy-start.1 = (bf16[256,1024]{1,0:T(8,128)(2,1)}, bf16[256,1024]{1,0:T(8,128)(2,1)S(1)}, u32[]{:S(2)}) copy-start(bf16[256,1024]{1,0:T(8,128)(2,1)S(1)} %collective-permute-done.8.v1) | copy-start | bytes 1572868
  27.2 14.1 %collective-permute-start.9 = (bf16[256,1024]{1,0:T(8,128)(2,1)S(1)}, bf16[256,1024]{1,0:T(8,128)(2,1)S(1)}, u32[]{:S(2)}, u32[]{:S(2)}) collective-permute-start(bf16[256,1024]{1,0:T(8,128)(2,1)S(1)} %get-tuple-element.10), channel_id=1, source_target_pairs={{0,4},{2,6},{4,0},{6,2},{8,12},{10,14},{12,8},{14,10},{16,20},{18,... | collective-permute-start | bytes 1572872 | tf_op jit(solution)/shard_map/ppermute | solution.py:143
  28.8 24.4 %collective-permute-start.1 = (bf16[256,1024]{1,0:T(8,128)(2,1)S(1)}, bf16[256,1024]{1,0:T(8,128)(2,1)S(1)}, u32[]{:S(2)}, u32[]{:S(2)}) collective-permute-start(bf16[256,1024]{1,0:T(8,128)(2,1)S(1)} %get-tuple-element.12), channel_id=1, source_target_pairs={{0,2},{2,0},{4,6},{6,4},{8,10},{10,8},{12,14},{14,12},{16,18},{18,... | collective-permute-start | bytes 1572872 | tf_op jit(solution)/shard_map/ppermute | solution.py:143
  31.3 23.6 %copy-start.7 = (bf16[256,1024]{1,0:T(8,128)(2,1)}, bf16[256,1024]{1,0:T(8,128)(2,1)S(1)}, u32[]{:S(2)}) copy-start(bf16[256,1024]{1,0:T(8,128)(2,1)S(1)} %collective-permute-done.2.k3) | copy-start | bytes 1572868
  31.3 22.0 %collective-permute-start.3 = (bf16[256,1024]{1,0:T(8,128)(2,1)S(1)}, bf16[256,1024]{1,0:T(8,128)(2,1)S(1)}, u32[]{:S(2)}, u32[]{:S(2)}) collective-permute-start(bf16[256,1024]{1,0:T(8,128)(2,1)S(1)} %collective-permute-done.2.k3), channel_id=1, source_target_pairs={{0,2},{2,0},{4,6},{6,4},{8,10},{10,8},{12,14},{14,12},{16,18},{18,... | collective-permute-start | bytes 1572872 | tf_op jit(solution)/shard_map/ppermute | solution.py:143
  35.5 31.2 %collective-permute-start.11 = (bf16[256,1024]{1,0:T(8,128)(2,1)S(1)}, bf16[256,1024]{1,0:T(8,128)(2,1)S(1)}, u32[]{:S(2)}, u32[]{:S(2)}) collective-permute-start(bf16[256,1024]{1,0:T(8,128)(2,1)S(1)} %get-tuple-element.9), channel_id=1, source_target_pairs={{0,2},{2,0},{4,6},{6,4},{8,10},{10,8},{12,14},{14,12},{16,18},{18,... | collective-permute-start | bytes 1572872 | tf_op jit(solution)/shard_map/ppermute | solution.py:143
  41.3 25.4 %copy-start.4 = (bf16[256,1024]{1,0:T(8,128)(2,1)}, bf16[256,1024]{1,0:T(8,128)(2,1)S(1)}, u32[]{:S(2)}) copy-start(bf16[256,1024]{1,0:T(8,128)(2,1)S(1)} %collective-permute-done.9.v3) | copy-start | bytes 1572868
  41.3 34.3 %collective-permute-start.10 = (bf16[256,1024]{1,0:T(8,128)(2,1)S(1)}, bf16[256,1024]{1,0:T(8,128)(2,1)S(1)}, u32[]{:S(2)}, u32[]{:S(2)}) collective-permute-start(bf16[256,1024]{1,0:T(8,128)(2,1)S(1)} %collective-permute-done.9.v3), channel_id=1, source_target_pairs={{0,2},{2,0},{4,6},{6,4},{8,10},{10,8},{12,14},{14,12},{16,18},{18,... | collective-permute-start | bytes 1572872 | tf_op jit(solution)/shard_map/ppermute | solution.py:143
  41.9 5.5 %collective-permute-start.4 = (s32[256]{0:T(256)S(1)}, s32[256]{0:T(256)S(1)}, u32[]{:S(2)}, u32[]{:S(2)}) collective-permute-start(s32[256]{0:T(256)S(1)} %bitcast.8), channel_id=1, source_target_pairs={{0,8},{2,10},{4,12},{6,14},{8,16},{10,18},{12,20},{14,22},{16,24},... | collective-permute-start | bytes 3080 | tf_op jit(solution)/shard_map/ppermute | solution.py:143
  47.3 7.5 %copy-start.6 = (s32[256]{0:T(256)}, s32[256]{0:T(256)S(1)}, u32[]{:S(2)}) copy-start(s32[256]{0:T(256)S(1)} %collective-permute-done.4) | copy-start | bytes 3076
  47.3 3.6 %collective-permute-start.6 = (s32[256]{0:T(256)S(1)}, s32[256]{0:T(256)S(1)}, u32[]{:S(2)}, u32[]{:S(2)}) collective-permute-start(s32[256]{0:T(256)S(1)} %get-tuple-element.13), channel_id=1, source_target_pairs={{0,4},{2,6},{4,0},{6,2},{8,12},{10,14},{12,8},{14,10},{16,20},{18,... | collective-permute-start | bytes 3080 | tf_op jit(solution)/shard_map/ppermute | solution.py:143
  50.9 3.9 %copy-start.10 = (s32[256]{0:T(256)}, s32[256]{0:T(256)S(1)}, u32[]{:S(2)}) copy-start(s32[256]{0:T(256)S(1)} %collective-permute-done.6) | copy-start | bytes 3076
  50.9 1.2 %collective-permute-start.5 = (s32[256]{0:T(256)S(1)}, s32[256]{0:T(256)S(1)}, u32[]{:S(2)}, u32[]{:S(2)}) collective-permute-start(s32[256]{0:T(256)S(1)} %get-tuple-element.14), channel_id=1, source_target_pairs={{0,2},{2,0},{4,6},{6,4},{8,10},{10,8},{12,14},{14,12},{16,18},{18,... | collective-permute-start | bytes 3080 | tf_op jit(solution)/shard_map/ppermute | solution.py:143
  52.1 2.8 %copy-start.11 = (s32[256]{0:T(256)}, s32[256]{0:T(256)S(1)}, u32[]{:S(2)}) copy-start(s32[256]{0:T(256)S(1)} %collective-permute-done.5) | copy-start | bytes 3076
  52.1 1.2 %collective-permute-start.7 = (s32[256]{0:T(256)S(1)}, s32[256]{0:T(256)S(1)}, u32[]{:S(2)}, u32[]{:S(2)}) collective-permute-start(s32[256]{0:T(256)S(1)} %collective-permute-done.6), channel_id=1, source_target_pairs={{0,2},{2,0},{4,6},{6,4},{8,10},{10,8},{12,14},{14,12},{16,18},{18,... | collective-permute-start | bytes 3080 | tf_op jit(solution)/shard_map/ppermute | solution.py:143
  53.2 1.6 %copy-start.12 = (s32[256]{0:T(256)}, s32[256]{0:T(256)S(1)}, u32[]{:S(2)}) copy-start(s32[256]{0:T(256)S(1)} %collective-permute-done.7) | copy-start | bytes 3076
  53.3 0.8 copy-start.8
  54.0 0.8 copy-start.9
  66.8 0.8 copy-start.2
  75.6 0.8 copy-start.5
